TPU v7x, 32 devices: a whole 2x2x4 slice. The times are simulated.
32 devices in a mesh: dp: 8 (over z, x), mp: 4 (over y, core).
Axes of the slice: x: 2, y: 2, z: 4, core: 2. Of those that a mesh axis runs over, the one named last changes fastest.
Arguments:
- patches: bfloat16 [4096, 2048], P('dp'), may hold values from -6 to 6
- cotangent: bfloat16 [4096, 8192], P('dp', 'mp'), may hold values from -0.09375 to 0.09375
- weight: float32 [2048, 8192], P('dp', 'mp'), may hold values from -0.125 to 0.125
- accum: float32 [2048, 8192], P('dp', 'mp'), may hold values from 0.1 to 4
Outputs:
- new_weight: float32 [2048, 8192], P(('dp', 'mp'))
- new_accum: float32 [2048, 8192], P(('dp', 'mp'))
- weight_copy: bfloat16 [2048, 8192], P(None, 'mp')
All inputs are finite; a program needn't handle non-finite values.
Results may differ from a plain program's by a relative error of at most 0.001.
Values may be sent and summed in bfloat16 or wider, within the bound.
A program may use at most 192 MiB of HBM per device.

v0:
```python
import jax
import jax.numpy as jnp
from jax import lax
from jax.sharding import PartitionSpec as P

learning_rate = 0.02


def adagrad(accum, weight, grad):
    summed = accum + grad * grad
    return (summed, weight - learning_rate * grad * lax.rsqrt(summed))


def shards(patches, cotangent, weight, accum):
    patch_block = lax.all_to_all(patches, "dp", split_axis=1, concat_axis=0, tiled=True)
    grad_block = jnp.einsum(
        "tr,tf->rf",
        patch_block,
        lax.all_gather(cotangent, "dp", axis=0, tiled=True),
        preferred_element_type=jnp.float32,
    )
    accum_block, weight_block = adagrad(accum, weight, grad_block)
    weight_copy = lax.all_gather(weight_block.astype(jnp.bfloat16), "dp", axis=0, tiled=True)
    new_accum, new_weight = (
        lax.all_to_all(accum_block, "mp", split_axis=0, concat_axis=1, tiled=True),
        lax.all_to_all(weight_block, "mp", split_axis=0, concat_axis=1, tiled=True),
    )
    return (new_weight, new_accum, weight_copy)


def solution(mesh):
    return jax.shard_map(
        shards,
        mesh=mesh,
        in_specs=(P("dp", None), P("dp", "mp"), P("dp", "mp"), P("dp", "mp")),
        out_specs=(P(("dp", "mp"), None), P(("dp", "mp"), None), P(None, "mp")),
        check_vma=False,
    )
```

profile of v0, /device:TPU:0, one launch (start us, length us, event | category | flops | bytes accessed | tf_op | source)
XLA Modules:
  0.0 430.2 jit_solution(2336489553796141500)
XLA Ops:
  7.2 0.0 all-gather.3.cloned.1.call-start
  7.2 0.7 all-gather.3.cloned.1.call-update
  7.9 0.0 all-gather.5.cloned.1.call-start
  7.9 2.9 copy.11
  10.8 107.2 %all_to_all.57 = bf16[512,8,256]{0,2,1:T(8,128)(2,1)} all-to-all(bf16[512,8,256]{0,2,1:T(8,128)(2,1)S(1)} %bitcast.18), channel_id=1, replica_groups=mesh['dp'=8,'mp'=4] {'dp'}, dimensions={1} | all-to-all | bytes 4194304 | tf_op jit(solution)/shard_map/all_to_all | solution.py:15
  118.0 2.8 copy.12
  120.9 158.3 %all-gather.3.cloned.1.call-done = bf16[4096,2048]{1,0:T(8,128)(2,1)} async-done(((bf16[512,2048]{1,0:T(8,128)(2,1)}), bf16[4096,2048]{1,0:T(8,128)(2,1)}) %all-gather.3.cloned.1.call-update) | async-done | bytes 16777232 | tf_op jit(solution)/shard_map/all_gather | solution.py:19
  279.1 12.9 %fusion = (bf16[256,2048]{1,0:T(8,128)(2,1)}, f32[256,2048]{1,0:T(8,128)}, f32[256,2048]{1,0:T(8,128)}) fusion(f32[256,2048]{1,0:T(8,128)} %param.6, f32[256,2048]{1,0:T(8,128)} %param.7, bf16[4096,256]{1,0:T(8,128)(2,1)S(1)} %bitcast.13, bf16[4096,2048]{1,0:T(8,128)(2,1)} %all-gather.3.cloned.1.call-done), kind=kOutput, calls=%fused_computation.2 | convolution fusion | flops 4298113024 | bytes 28311552 | tf_op jit(solution)/shard_map/tr,tf->rf/dot_general | solution.py:16
  292.0 0.0 all-gather.5.cloned.1.call-update
  292.1 30.2 %all_to_all.58 = f32[4,64,2048]{2,1,0:T(8,128)} all-to-all(f32[4,64,2048]{2,1,0:T(8,128)} %bitcast.14), channel_id=1, replica_groups=mesh['dp'=8,'mp'=4] {'mp'}, dimensions={0} | all-to-all | bytes 4194304 | tf_op jit(solution)/shard_map/all_to_all | solution.py:26
  322.2 3.6 all-to-all-start.2
  325.8 3.1 copy.15
  329.0 22.5 %all-to-all-done.2 = f32[4,64,2048]{2,1,0:T(8,128)S(1)} async-done(((f32[4,64,2048]{2,1,0:T(8,128)}), f32[4,64,2048]{2,1,0:T(8,128)S(1)}, u32[]{:S(2)}, u32[]{:S(2)}) %all-to-all-start.2) | async-done | bytes 2097184 | tf_op jit(solution)/shard_map/all_to_all | solution.py:25
  351.5 1.5 copy.16
  352.9 61.9 %all-gather.5.cloned.1.call-done = bf16[2048,2048]{1,0:T(8,128)(2,1)} async-done(((bf16[256,2048]{1,0:T(8,128)(2,1)}), bf16[2048,2048]{1,0:T(8,128)(2,1)}) %all-gather.5.cloned.1.call-update) | async-done | bytes 8388624 | tf_op jit(solution)/shard_map/all_gather | solution.py:23
  414.9 8.4 %copy.18 = bf16[2048,2048]{1,0:T(8,128)(2,1)} copy(bf16[2048,2048]{1,0:T(8,128)(2,1)} %all-gather.5.cloned.1.call-done) | data formatting | bytes 16777216
Async XLA Ops:
  7.2 272.0 %all-gather.3.cloned.1.call-start = ((), (), s32[]{:S(2)}) async-start(), calls=%async_computation.3 | async-start | bytes 18874368 | tf_op jit(solution)/shard_map/all_gather | solution.py:19
  7.9 407.0 %all-gather.5.cloned.1.call-start = ((), (), s32[]{:S(2)}) async-start(), calls=%async_computation.4 | async-start | bytes 9437184 | tf_op jit(solution)/shard_map/all_gather | solution.py:23
  322.2 29.3 %all-to-all-start.2 = ((f32[4,64,2048]{2,1,0:T(8,128)}), f32[4,64,2048]{2,1,0:T(8,128)S(1)}, u32[]{:S(2)}, u32[]{:S(2)}) async-start(f32[4,64,2048]{2,1,0:T(8,128)} %bitcast.5), calls=%async_computation.2 | async-start | bytes 4194304 | tf_op jit(solution)/shard_map/all_to_all | solution.py:25
Sparse Core Ops, SparseCore 0:
  10.1 268.9 all-gather.2
  292.2 122.6 all-gather.4
where the time goes:
time: 431 us; the launch traced here: 430 us
  waiting for transfers between devices  243 us (56%)
  blocking collectives  137 us (32%)
  local copies, waits for them, and re-layouts  18.8 us (4%)
  between operations  14.1 us (3%)
  matrix products  12.9 us (3%)
    all_gather x1, waiting for transfers between devices, shards(): lax.all_gather(cotangent, 'dp', axis=0, tiled=True)  158 us
    all_to_all x1, blocking collectives, shards(): lax.all_to_all(patches, 'dp', split_axis=1, concat_axis=0, tiled=True)  107 us
    all_gather x1, waiting for transfers between devices, shards(): lax.all_gather(weight_block.astype(jnp.bfloat16), 'dp', axis=0, tiled=True)  61.9 us
    all_to_all x1, blocking collectives, shards(): lax.all_to_all(weight_block, 'mp', split_axis=0, concat_axis=1, tiled=True)  30.2 us
    all_to_all x1, waiting for transfers between devices, shards(): lax.all_to_all(accum_block, 'mp', split_axis=0, concat_axis=1, tiled=True)  22.5 us
    dot_general x1, matrix products, shards(): jnp.einsum('tr,tf->rf', patch_block, lax.all_gather(cotangent, 'dp', axis...  12.9 us
    unnamed x2, local copies, waits for them, and re-layouts  11.3 us
  transfers between devices with their start and end apart: 3, of which 3 were waited for; matrix products, arithmetic and copies ran while one was open for 2% of the time, Pallas kernels for 0%

commit v1 on v0

--- a/solution.py
+++ b/solution.py
@@ -4,6 +4,29 @@
 from jax.sharding import PartitionSpec as P
 
 learning_rate = 0.02
+
+
+def in_blocks(shard, dim, count):
+    lengths = shard.shape
+    tiles = shard.reshape(*lengths[:dim], count, lengths[dim] // count, *lengths[dim + 1 :])
+    return jnp.moveaxis(tiles, dim, 0)
+
+
+def in_order(blocks, dim):
+    lengths = list(blocks.shape[1:])
+    lengths[dim] *= blocks.shape[0]
+    return jnp.moveaxis(blocks, 0, dim).reshape(lengths)
+
+
+def sent_to_each(x, axis, split_dim, concat_dim):
+    peers, index = (lax.axis_size(axis), lax.axis_index(axis))
+    pieces = in_blocks(x, split_dim, peers)
+    outs = [pieces[index]]
+    for step in range(1, peers):
+        sent = pieces[(index + step) % peers]
+        outs.append(lax.ppermute(sent, axis, [(i, (i + step) % peers) for i in range(peers)]))
+    pieces = jnp.stack(outs)[(index - jnp.arange(peers)) % peers]
+    return in_order(pieces, concat_dim)
 
 
 def adagrad(accum, weight, grad):
@@ -22,7 +45,7 @@
     accum_block, weight_block = adagrad(accum, weight, grad_block)
     weight_copy = lax.all_gather(weight_block.astype(jnp.bfloat16), "dp", axis=0, tiled=True)
     new_accum, new_weight = (
-        lax.all_to_all(accum_block, "mp", split_axis=0, concat_axis=1, tiled=True),
+        sent_to_each(accum_block, "mp", 0, 1),
         lax.all_to_all(weight_block, "mp", split_axis=0, concat_axis=1, tiled=True),
     )
     return (new_weight, new_accum, weight_copy)

time: 431 us -> 431 us (level)
  blocking collectives: 137 us -> 107 us
  waiting for transfers between devices: 243 us -> 266 us
    ppermute x0 -> x3, waiting for transfers between devices: none -> 45.6 us  [sent_to_each(): lax.ppermute(sent, axis, [(i, (i + step) % peers) for i in range(peers)])]
    all_to_all x1 -> x0, blocking collectives: 30.2 us -> none  [shards(): lax.all_to_all(weight_block, 'mp', split_axis=0, concat_axis=1, tiled=True)]
    all_to_all x1, waiting for transfers between devices: 22.5 us -> 0.01 us  [shards(): lax.all_to_all(weight_block, 'mp', split_axis=0, concat_axis=1, tiled=True)]
    unnamed x2 -> x4, local copies, waits for them, and re-layouts: 11.3 us -> 11.3 us
  transfers between devices with their start and end apart: 3 -> 6, of which waited for: 3 -> 4; matrix products, arithmetic and copies ran while one was open for 2% -> 3% of each run, Pallas kernels for 0% -> 0%
where the time goes in v1:
time: 431 us; the launch traced here: 430 us
  waiting for transfers between devices  266 us (62%)
  blocking collectives  107 us (25%)
  local copies, waits for them, and re-layouts  22.7 us (5%)
  between operations  14.1 us (3%)
  matrix products  12.9 us (3%)
  starting transfers between devices  6.91 us (2%)
    all_gather x1, waiting for transfers between devices, shards(): lax.all_gather(cotangent, 'dp', axis=0, tiled=True)  158 us
    all_to_all x1, blocking collectives, shards(): lax.all_to_all(patches, 'dp', split_axis=1, concat_axis=0, tiled=True)  107 us
    all_gather x1, waiting for transfers between devices, shards(): lax.all_gather(weight_block.astype(jnp.bfloat16), 'dp', axis=0, tiled=True)  61.6 us
    ppermute x3, waiting for transfers between devices, sent_to_each(): lax.ppermute(sent, axis, [(i, (i + step) % peers) for i in range(peers)])  45.6 us
    dot_general x1, matrix products, shards(): jnp.einsum('tr,tf->rf', patch_block, lax.all_gather(cotangent, 'dp', axis...  12.9 us
    unnamed x4, local copies, waits for them, and re-layouts  11.3 us
  transfers between devices with their start and end apart: 6, of which 4 were waited for; matrix products, arithmetic and copies ran while one was open for 3% of the time, Pallas kernels for 0%

profile of v1, /device:TPU:0, one launch (start us, length us, event | category | flops | bytes accessed | tf_op | source)
XLA Modules:
  0.0 430.1 jit_solution(9466205077020851405)
XLA Ops:
  7.2 0.0 all-gather.3.cloned.1.call-start
  7.2 0.7 all-gather.3.cloned.1.call-update
  7.9 0.0 all-gather.5.cloned.1.call-start
  7.9 2.9 copy.11
  10.8 107.2 %all_to_all.38 = bf16[512,8,256]{0,2,1:T(8,128)(2,1)} all-to-all(bf16[512,8,256]{0,2,1:T(8,128)(2,1)S(1)} %bitcast.29), channel_id=1, replica_groups=mesh['dp'=8,'mp'=4] {'dp'}, dimensions={1} | all-to-all | bytes 4194304 | tf_op jit(solution)/shard_map/all_to_all | solution.py:38
  118.0 2.8 copy.12
  120.9 158.3 %all-gather.3.cloned.1.call-done = bf16[4096,2048]{1,0:T(8,128)(2,1)} async-done(((bf16[512,2048]{1,0:T(8,128)(2,1)}), bf16[4096,2048]{1,0:T(8,128)(2,1)}) %all-gather.3.cloned.1.call-update) | async-done | bytes 16777232 | tf_op jit(solution)/shard_map/all_gather | solution.py:42
  279.1 12.9 %fusion.2 = (bf16[256,2048]{1,0:T(8,128)(2,1)}, f32[256,2048]{1,0:T(8,128)}, f32[256,2048]{1,0:T(8,128)}) fusion(f32[256,2048]{1,0:T(8,128)} %param.6, f32[256,2048]{1,0:T(8,128)} %param.7, bf16[4096,256]{1,0:T(8,128)(2,1)S(1)} %bitcast.24, bf16[4096,2048]{1,0:T(8,128)(2,1)} %all-gather.3.cloned.1.call-done), kind=kOutput, calls=%fused_computation.15 | convolution fusion | flops 4298113024 | bytes 28311552 | tf_op jit(solution)/shard_map/tr,tf->rf/dot_general | solution.py:39
  292.0 0.0 all-gather.5.cloned.1.call-update
  292.1 0.0 copy-start
  292.1 4.6 %all-to-all-start.1 = ((f32[4,64,2048]{2,1,0:T(8,128)}), f32[4,64,2048]{2,1,0:T(8,128)}, u32[]{:S(2)}, u32[]{:S(2)}) async-start(f32[4,64,2048]{2,1,0:T(8,128)} %bitcast.25), calls=%async_computation.1 | async-start | bytes 4194304 | tf_op jit(solution)/shard_map/all_to_all | solution.py:49
  296.8 0.0 copy-done
  296.8 0.2 constant_dynamic-slice_fusion
  297.0 1.7 collective-permute-start.2
  298.7 0.4 collective-permute-start.1
  299.1 0.1 collective-permute-start
  299.2 32.5 %collective-permute-done.2 = f32[64,2048]{1,0:T(8,128)S(1)} collective-permute-done((f32[64,2048]{1,0:T(8,128)S(1)}, f32[64,2048]{1,0:T(8,128)S(1)}, u32[]{:S(2)}, u32[]{:S(2)}) %collective-permute-start.2) | collective-permute-done | bytes 524320 | tf_op jit(solution)/shard_map/ppermute | solution.py:27
  331.7 13.1 %collective-permute-done.1 = f32[64,2048]{1,0:T(8,128)S(1)} collective-permute-done((f32[64,2048]{1,0:T(8,128)S(1)}, f32[64,2048]{1,0:T(8,128)S(1)}, u32[]{:S(2)}, u32[]{:S(2)}) %collective-permute-start.1) | collective-permute-done | bytes 524320 | tf_op jit(solution)/shard_map/ppermute | solution.py:27
  344.8 0.0 collective-permute-done
  344.8 0.2 pad_maximum_fusion
  345.0 2.0 gather_fusion
  347.0 3.1 copy.16
  350.2 0.0 all-to-all-done.1
  350.2 3.1 copy.15
  353.3 61.6 %all-gather.5.cloned.1.call-done = bf16[2048,2048]{1,0:T(8,128)(2,1)} async-done(((bf16[256,2048]{1,0:T(8,128)(2,1)}), bf16[2048,2048]{1,0:T(8,128)(2,1)}) %all-gather.5.cloned.1.call-update) | async-done | bytes 8388624 | tf_op jit(solution)/shard_map/all_gather | solution.py:46
  414.9 8.4 %copy.18 = bf16[2048,2048]{1,0:T(8,128)(2,1)} copy(bf16[2048,2048]{1,0:T(8,128)(2,1)} %all-gather.5.cloned.1.call-done) | data formatting | bytes 16777216
  (2 shorter events, 0.0 us)
Async XLA Ops:
  7.2 272.0 %all-gather.3.cloned.1.call-start = ((), (), s32[]{:S(2)}) async-start(), calls=%async_computation.2 | async-start | bytes 18874368 | tf_op jit(solution)/shard_map/all_gather | solution.py:42
  7.9 407.0 %all-gather.5.cloned.1.call-start = ((), (), s32[]{:S(2)}) async-start(), calls=%async_computation.3 | async-start | bytes 9437184 | tf_op jit(solution)/shard_map/all_gather | solution.py:46
  292.1 4.7 %copy-start = (f32[256,2048]{1,0:T(8,128)S(1)}, f32[256,2048]{1,0:T(8,128)}, u32[]{:S(2)}) copy-start(f32[256,2048]{1,0:T(8,128)} %get-tuple-element.5) | copy-start | bytes 6291460
  292.1 58.1 %all-to-all-start.1 = ((f32[4,64,2048]{2,1,0:T(8,128)}), f32[4,64,2048]{2,1,0:T(8,128)}, u32[]{:S(2)}, u32[]{:S(2)}) async-start(f32[4,64,2048]{2,1,0:T(8,128)} %bitcast.25), calls=%async_computation.1 | async-start | bytes 4194304 | tf_op jit(solution)/shard_map/all_to_all | solution.py:49
  297.0 34.7 %collective-permute-start.2 = (f32[64,2048]{1,0:T(8,128)S(1)}, f32[64,2048]{1,0:T(8,128)S(1)}, u32[]{:S(2)}, u32[]{:S(2)}) collective-permute-start(f32[64,2048]{1,0:T(8,128)S(1)} %get-tuple-element.7), channel_id=1, source_target_pairs={{0,3},{1,0},{2,1},{3,2},{4,7},{5,4},{6,5},{7,6},{8,11},{9,8},{10,9... | collective-permute-start | bytes 1572872 | tf_op jit(solution)/shard_map/ppermute | solution.py:27
  298.7 46.1 %collective-permute-start.1 = (f32[64,2048]{1,0:T(8,128)S(1)}, f32[64,2048]{1,0:T(8,128)S(1)}, u32[]{:S(2)}, u32[]{:S(2)}) collective-permute-start(f32[64,2048]{1,0:T(8,128)S(1)} %get-tuple-element.8), channel_id=1, source_target_pairs={{0,2},{1,3},{2,0},{3,1},{4,6},{5,7},{6,4},{7,5},{8,10},{9,11},{10,... | collective-permute-start | bytes 1572872 | tf_op jit(solution)/shard_map/ppermute | solution.py:27
  299.1 45.7 %collective-permute-start = (f32[64,2048]{1,0:T(8,128)S(1)}, f32[64,2048]{1,0:T(8,128)S(1)}, u32[]{:S(2)}, u32[]{:S(2)}) collective-permute-start(f32[64,2048]{1,0:T(8,128)S(1)} %get-tuple-element.9), channel_id=1, source_target_pairs={{0,1},{1,2},{2,3},{3,0},{4,5},{5,6},{6,7},{7,4},{8,9},{9,10},{10,1... | collective-permute-start | bytes 1572872 | tf_op jit(solution)/shard_map/ppermute | solution.py:27
Sparse Core Ops, SparseCore 0:
  10.1 268.9 all-gather.2
  292.2 122.6 all-gather.4
